TPU v7x, 32 devices: a whole 2x2x4 slice. The times are simulated.
32 devices in a mesh: dp: 2 (over x), col: 4 (over z), row: 4 (over y, core).
Axes of the slice: x: 2, y: 2, z: 4, core: 2. Of those that a mesh axis runs over, the one named last changes fastest.
Arguments:
- x_tok: bfloat16 [16384, 4096], P(('dp', 'row'), 'col'), parts along dimension 0
- ln_gamma: float32 [4096], P('col')
- w_in: bfloat16 [4096, 16384], P('row', 'col')
- w_out: bfloat16 [16384, 4096], P('row', 'col')
Outputs:
- output: bfloat16 [16384, 4096], P(('dp', 'row'), 'col'), parts along dimension 0
There are 2 independent parts. A program takes and returns all parts, laid end to end along the dimension named above; an argument that names none is the same for every part.
All inputs are finite; a program needn't handle non-finite values.
Results may differ from a plain program's by a relative error of at most 0.001.
Values are sent between devices in bfloat16 or wider.
A program may use at most 1 GiB of HBM per device.

v0:
```python
import jax
import jax.numpy as jnp
from jax import lax
from jax.sharding import PartitionSpec as P

LN_EPS = 1e-5


def solution(mesh):
    col_size = mesh.shape["col"]
    tok_spec = P(("dp", "row"), "col")

    def local_block(x_loc, gamma_loc, w_in_loc, w_out_loc):
        d_model = x_loc.shape[1] * col_size
        x_f32 = x_loc.astype(jnp.float32)
        part_sums = jnp.concatenate([jnp.sum(x_f32, axis=1, keepdims=True), jnp.sum(x_f32 * x_f32, axis=1, keepdims=True)], axis=1)
        row_sums = lax.psum(part_sums, "col")
        mean_row = row_sums[:, 0:1] / d_model
        var_row = row_sums[:, 1:2] / d_model - mean_row * mean_row
        normed = ((x_f32 - mean_row) * lax.rsqrt(var_row + LN_EPS) * gamma_loc).astype(jnp.bfloat16)
        z_panel = lax.all_gather(normed, "col", axis=1, tiled=True)
        w_in_panel = lax.all_gather(w_in_loc, "row", axis=0, tiled=True)
        pre_act = jnp.dot(z_panel, w_in_panel, preferred_element_type=jnp.float32)
        hidden = jax.nn.gelu(pre_act, approximate=True).astype(jnp.bfloat16)
        h_panel = lax.all_gather(hidden, "col", axis=1, tiled=True)
        w_out_panel = lax.all_gather(w_out_loc, "row", axis=0, tiled=True)
        branch = jnp.dot(h_panel, w_out_panel, preferred_element_type=jnp.float32)
        return (x_f32 + branch).astype(jnp.bfloat16)

    return jax.shard_map(local_block, mesh=mesh, in_specs=(tok_spec, P("col"), P("row", "col"), P("row", "col")), out_specs=tok_spec, check_vma=False)
```

profile of v0, /device:TPU:0, one launch (start us, length us, event | category | flops | bytes accessed | tf_op | source)
XLA Modules:
  0.0 1925.7 jit_solution(12248197463331606712)
XLA Ops:
  6.5 0.0 all-gather.5.cloned.1.call-start
  6.5 3.4 convert_reduce_fusion
  10.0 20.5 %psum.7 = f32[2048,2]{0,1:T(2,128)S(1)} all-reduce(f32[2048,2]{0,1:T(2,128)S(1)} %pad_maximum_fusion), channel_id=1, replica_groups=mesh['dp'=2,'col'=4,'row'=4] {'col'}, use_global_device_ids=true, to_apply=%region_2.0 | all-reduce | flops 4096 | bytes 32768 | tf_op jit(solution)/shard_map/psum | solution.py:17
  30.6 4.3 fusion.11
  34.9 0.0 all-gather.5.cloned.1.call-update
  34.9 0.0 all-gather.7.cloned.1.call-start
  35.0 0.7 all-gather.7.cloned.1.call-update
  35.7 0.0 all-gather.11.cloned.1.call-start
  35.7 0.7 all-gather.11.cloned.1.call-update
  36.4 0.0 all-gather.9.cloned.1.call-start
  36.4 284.6 %all-gather.5.cloned.1.call-done = bf16[2048,4096]{1,0:T(8,128)(2,1)} async-done(((bf16[2048,1024]{1,0:T(8,128)(2,1)}), bf16[2048,4096]{1,0:T(8,128)(2,1)}) %all-gather.5.cloned.1.call-update) | async-done | bytes 16777232 | tf_op jit(solution)/shard_map/all_gather | solution.py:21
  321.0 201.9 %all-gather.7.cloned.1.call-done = bf16[4096,4096]{1,0:T(8,128)(2,1)} async-done(((bf16[1024,4096]{1,0:T(8,128)(2,1)}), bf16[4096,4096]{1,0:T(8,128)(2,1)}) %all-gather.7.cloned.1.call-update) | async-done | bytes 33554448 | tf_op jit(solution)/shard_map/all_gather | solution.py:22
  522.9 87.7 %fusion.7 = bf16[2048,4096]{1,0:T(8,128)(2,1)} fusion(bf16[2048,4096]{1,0:T(8,128)(2,1)} %all-gather.5.cloned.1.call-done, bf16[4096,4096]{1,0:T(8,128)(2,1)} %all-gather.7.cloned.1.call-done), kind=kOutput, calls=%fused_computation.8 | convolution fusion | flops 68794974208 | bytes 67108864 | tf_op jit(solution)/shard_map/dot_general | solution.py:23
  610.7 0.0 all-gather.9.cloned.1.call-update
  610.7 116.0 %all-gather.11.cloned.1.call-done = bf16[16384,1024]{1,0:T(8,128)(2,1)} async-done(((bf16[4096,1024]{1,0:T(8,128)(2,1)}), bf16[16384,1024]{1,0:T(8,128)(2,1)}) %all-gather.11.cloned.1.call-update) | async-done | bytes 33554448 | tf_op jit(solution)/shard_map/all_gather | solution.py:26
  726.7 1113.2 %all-gather.9.cloned.1.call-done = bf16[2048,16384]{1,0:T(8,128)(2,1)} async-done(((bf16[2048,4096]{1,0:T(8,128)(2,1)}), bf16[2048,16384]{1,0:T(8,128)(2,1)}) %all-gather.9.cloned.1.call-update) | async-done | bytes 67108880 | tf_op jit(solution)/shard_map/all_gather | solution.py:25
  1839.9 79.3 %fusion.12 = bf16[2048,1024]{1,0:T(8,128)(2,1)} fusion(bf16[2048,1024]{1,0:T(8,128)(2,1)} %param.4, bf16[2048,16384]{1,0:T(8,128)(2,1)} %all-gather.9.cloned.1.call-done, bf16[16384,1024]{1,0:T(8,128)(2,1)} %all-gather.11.cloned.1.call-done), kind=kOutput, calls=%fused_computation.17 | convolution fusion | flops 68725768192 | bytes 109051904 | tf_op jit(solution)/shard_map/dot_general | solution.py:27
  (2 shorter events, 0.0 us)
Async XLA Ops:
  6.5 314.5 %all-gather.5.cloned.1.call-start = ((), (), s32[]{:S(2)}) async-start(), calls=%async_computation | async-start | bytes 20971520 | tf_op jit(solution)/shard_map/all_gather | solution.py:21
  34.9 488.0 %all-gather.7.cloned.1.call-start = ((), (), s32[]{:S(2)}) async-start(), calls=%async_computation.1 | async-start | bytes 41943040 | tf_op jit(solution)/shard_map/all_gather | solution.py:22
  35.7 691.0 %all-gather.11.cloned.1.call-start = ((), (), s32[]{:S(2)}) async-start(), calls=%async_computation.3 | async-start | bytes 41943040 | tf_op jit(solution)/shard_map/all_gather | solution.py:26
  36.4 1803.5 %all-gather.9.cloned.1.call-start = ((), (), s32[]{:S(2)}) async-start(), calls=%async_computation.2 | async-start | bytes 83886080 | tf_op jit(solution)/shard_map/all_gather | solution.py:25
Sparse Core Ops, SparseCore 0:
  35.0 285.9 all-gather.4
  322.6 200.2 all-gather.6
  524.5 202.1 all-gather.10
  728.1 1111.7 all-gather.8
where the time goes:
time: 1930 us
  waiting for transfers between devices  1720 us (89%)
  matrix products  167 us (9%)
  blocking collectives  20.5 us (1%)
    all_gather x1, waiting for transfers between devices, local_block(): h_panel = lax.all_gather(hidden, 'col', axis=1, tiled=True)  1110 us
    all_gather x1, waiting for transfers between devices, local_block(): z_panel = lax.all_gather(normed, 'col', axis=1, tiled=True)  285 us
    all_gather x1, waiting for transfers between devices, local_block(): w_in_panel = lax.all_gather(w_in_loc, 'row', axis=0, tiled=True)  202 us
    all_gather x1, waiting for transfers between devices, local_block(): w_out_panel = lax.all_gather(w_out_loc, 'row', axis=0, tiled=True)  116 us
    dot_general x1, matrix products, local_block(): pre_act = jnp.dot(z_panel, w_in_panel, preferred_element_type=jnp.float32)  87.7 us
    dot_general x1, matrix products, local_block(): branch = jnp.dot(h_panel, w_out_panel, preferred_element_type=jnp.float32)  79.3 us
  transfers between devices with their start and end apart: 4, of which 4 were waited for; matrix products, arithmetic and copies ran while one was open for 5% of the time, Pallas kernels for 0%

commit v1 on v0

v1 whole, which is shorter than its diff:
```python
import jax
import jax.numpy as jnp
from jax import lax
from jax.experimental import pallas as pl
from jax.experimental.pallas import tpu as pltpu
from jax.sharding import PartitionSpec as P

LN_EPS = 1e-5
CHUNKS = 4
MESH = pl.DeviceIdType.MESH


def mlp_kernel(x_ref, gam_ref, w1_ref, w2_ref,
               y_ref, xg, w1g, w2g, pb, rb,
               lhs, wv, xs, pst, st_a, st_b, yst, gamv,
               xs_r, xs_l, x_rv, g_sd, g_rv,
               w1_so, w1_ro, w1_sy, w1_sx, w1_sd, w1_rv,
               w2_sz, w2_sy, w2_sx, w2_sd, w2_rv,
               rs_sd, rs_rv, wsem, lsem):
    n_tok, d_loc = x_ref.shape
    d_hid = w1_ref.shape[1]
    d_model = 4 * d_loc
    tc = n_tok // CHUNKS
    tile = wv.shape[2]
    n_h = d_hid // tile
    n_p = d_loc // tile
    steps = n_h + 4 * n_p
    w1_rows = w1_ref.shape[0] // 8
    w2_rows = w2_ref.shape[0] // 8

    xi = lax.axis_index("dp")
    z = lax.axis_index("col")
    row = lax.axis_index("row")
    yi = row // 2
    k = row % 2
    right, left = {"col": z + 1}, {"col": z - 1}
    partner = {"row": 2 * yi + 1 - k}
    y_nb = {"row": 2 * (1 - yi) + k}
    x_nb = {"dp": 1 - xi}

    def rc(src, dst, ssem, rsem, dev):
        return pltpu.make_async_remote_copy(src_ref=src, dst_ref=dst, send_sem=ssem, recv_sem=rsem,
                                            device_id=dev, device_id_type=MESH)

    def arrived(dst, rsem):
        rc(dst, dst, lsem.at[0], rsem, partner).wait_recv()

    def start(d):
        d.start()

    def drain(d):
        d.wait_send()

    def rows(c):
        return pl.ds(pl.multiple_of(c * tc, tc), tc)

    def x_own(c, act):
        @pl.when(z < 3)
        def _():
            act(rc(x_ref.at[rows(c)], xg.at[z, rows(c)], xs_r.at[z, c], x_rv.at[z, c], right))

        @pl.when(z > 0)
        def _():
            act(rc(x_ref.at[rows(c)], xg.at[z, rows(c)], xs_l.at[z, c], x_rv.at[z, c], left))

    def x_fwd(c, dist, act, wait):
        @pl.when(z - dist >= 0)
        def _():
            s = z - dist
            ref = xg.at[s, rows(c)]
            if wait:
                arrived(ref, x_rv.at[s, c])

            @pl.when(z < 3)
            def _():
                act(rc(ref, ref, xs_r.at[s, c], x_rv.at[s, c], right))

        @pl.when(z + dist <= 3)
        def _():
            s = z + dist
            ref = xg.at[s, rows(c)]
            if wait:
                arrived(ref, x_rv.at[s, c])

            @pl.when(z > 0)
            def _():
                act(rc(ref, ref, xs_l.at[s, c], x_rv.at[s, c], left))

    def gamma_sends(act):
        for d in range(1, 4):
            o = lax.rem(z + d, 4)
            act(rc(gam_ref, gamv.at[z], g_sd.at[d], g_rv.at[z], {"col": o}))

    def w1_ref_of(blk, sub):
        return w1g.at[blk, pl.ds(pl.multiple_of(sub * w1_rows, w1_rows), w1_rows)]

    def w1_own(act):
        for s in range(4):
            sub = xi * 4 + s
            src = w1_ref.at[pl.ds(pl.multiple_of(sub * w1_rows, w1_rows), w1_rows)]
            act(rc(src, w1_ref_of(row, sub), w1_sy.at[s], w1_rv.at[row, sub], y_nb))
        act(rc(w1_ref, w1g.at[row], w1_so.at[0], w1_ro.at[0], partner))

    def w1_y(s, act, wait):
        blk, sub = 2 * (1 - yi) + k, xi * 4 + s
        ref = w1_ref_of(blk, sub)
        if wait:
            arrived(ref, w1_rv.at[blk, sub])
        act(rc(ref, ref, w1_sx.at[s], w1_rv.at[blk, sub], x_nb))
        act(rc(ref, ref, w1_sd.at[sub], w1_rv.at[blk, sub], partner))

    def w1_x(s, act, wait):
        blk, sub = 2 * (1 - yi) + k, (1 - xi) * 4 + s
        ref = w1_ref_of(blk, sub)
        if wait:
            arrived(ref, w1_rv.at[blk, sub])
        act(rc(ref, ref, w1_sd.at[sub], w1_rv.at[blk, sub], partner))

    def w2_rows_of(sub):
        return pl.ds(pl.multiple_of(sub * w2_rows, w2_rows), w2_rows)

    def w2_src(s, act, first):
        sub = xi * 4 + s
        src, dst = w2_ref.at[w2_rows_of(sub)], w2g.at[z, w2_rows_of(sub)]
        here = jnp.logical_and(row == z, k == s % 2)

        @pl.when(jnp.logical_not(here))
        def _():
            act(rc(src, dst, w2_sz.at[s], w2_rv.at[z, sub], {"row": 2 * yi + s % 2, "col": row}))

        if first:
            @pl.when(here)
            def _():
                pltpu.make_async_copy(src, dst, w2_rv.at[z, sub]).start()

    def j_of(i):
        return jnp.where(z < 2, 3 - i, i)

    def w2_a(i, act, wait):
        j = j_of(i)
        for q in range(2):
            s = 2 * q + k
            sub = xi * 4 + s
            ref = w2g.at[j, w2_rows_of(sub)]
            if wait:
                arrived(ref, w2_rv.at[j, sub])

            @pl.when(yi == z // 2)
            def _():
                act(rc(ref, ref, w2_sy.at[j, q], w2_rv.at[j, sub], y_nb))

            act(rc(ref, ref, w2_sx.at[j, q], w2_rv.at[j, sub], x_nb))
            act(rc(ref, ref, w2_sd.at[j, sub], w2_rv.at[j, sub], partner))

    def w2_b(i, act, wait):
        j = j_of(i)
        for q in range(2):
            sub = (1 - xi) * 4 + 2 * q + k
            ref = w2g.at[j, w2_rows_of(sub)]
            if wait:
                arrived(ref, w2_rv.at[j, sub])
            act(rc(ref, ref, w2_sd.at[j, sub], w2_rv.at[j, sub], partner))

    def w2_c(i):
        j = j_of(i)
        for h in range(2):
            for q in range(2):
                sub = h * 4 + 2 * q + 1 - k
                arrived(w2g.at[j, w2_rows_of(sub)], w2_rv.at[j, sub])

    def p_send(c, dr, dest, act):
        act(rc(pb.at[dest, rows(c)], rb.at[dr, dest, rows(c)], rs_sd.at[dr, dest, c],
               rs_rv.at[dr, dest, c], {"col": z + 1 - 2 * dr}))

    def load(src, dst, sem):
        d = pltpu.make_async_copy(src, dst, lsem.at[sem])
        d.start()
        return d

    def inner(e):
        m = z == 1
        if e == 0:
            return jnp.where(m, 0, 1), jnp.where(m, 3, 0)
        if e == 1:
            return jnp.where(m, 0, 1), jnp.where(m, 2, 1)
        return jnp.where(m, 1, 0), jnp.where(m, 0, 3)

    def p_relay(c):
        @pl.when(jnp.logical_or(z == 1, z == 2))
        def _():
            for e in range(3):
                dr, dest = inner(e)
                arrived(rb.at[dr, dest, rows(c)], rs_rv.at[dr, dest, c])
                d1 = load(rb.at[dr, dest, rows(c)], st_a, 1)
                d2 = load(pb.at[dest, rows(c)], st_b, 2)
                d1.wait()
                d2.wait()
                st_a[...] = st_a[...] + st_b[...]
                load(st_a, pb.at[dest, rows(c)], 1).wait()
                p_send(c, dr, dest, start)

    def finish(c):
        d1 = load(pb.at[z, rows(c)], st_a, 1)
        d2 = load(x_ref.at[rows(c)], yst, 2)
        d1.wait()
        d2.wait()

        @pl.when(z > 0)
        def _():
            arrived(rb.at[0, z, rows(c)], rs_rv.at[0, z, c])
            load(rb.at[0, z, rows(c)], st_b, 1).wait()
            st_a[...] = st_a[...] + st_b[...]

        @pl.when(z < 3)
        def _():
            arrived(rb.at[1, z, rows(c)], rs_rv.at[1, z, c])
            load(rb.at[1, z, rows(c)], st_b, 1).wait()
            st_a[...] = st_a[...] + st_b[...]

        yst[...] = (yst[...].astype(jnp.float32) + st_a[...]).astype(jnp.bfloat16)
        load(yst, y_ref.at[rows(c)], 1).wait()

    def normalise(c):
        for s in range(4):
            @pl.when(z == s)
            def _():
                pltpu.make_async_copy(x_ref.at[rows(c)], xs.at[s], lsem.at[3]).start()

            @pl.when(z != s)
            def _():
                pltpu.make_async_copy(xg.at[s, rows(c)], xs.at[s], lsem.at[3]).start()
        pltpu.make_async_copy(xg.at[:, rows(c)], xs, lsem.at[3]).wait()
        blk = 64

        def part(r, carry):
            rr = pl.ds(pl.multiple_of(r * blk, blk), blk)
            tot = jnp.zeros((blk, 1), jnp.float32)
            sq = jnp.zeros((blk, 1), jnp.float32)
            for s in range(4):
                v = xs[s, rr, :].astype(jnp.float32)
                tot = tot + jnp.sum(v, axis=1, keepdims=True)
                sq = sq + jnp.sum(v * v, axis=1, keepdims=True)
            mean = tot / d_model
            var = sq / d_model - mean * mean
            inv = lax.rsqrt(var + LN_EPS)
            for s in range(4):
                v = xs[s, rr, :].astype(jnp.float32)
                lhs[0, rr, s * d_loc:(s + 1) * d_loc] = ((v - mean) * inv * gamv[s]).astype(jnp.bfloat16)
            return carry

        lax.fori_loop(0, tc // blk, part, 0)

    def w_start(u, slot):
        cols = pl.ds(pl.multiple_of(lax.rem(u, n_h) * tile, tile), tile)

        @pl.when(u < n_h)
        def _():
            r = w1_ref.shape[0]
            for b in range(4):
                dst = wv.at[slot, pl.ds(b * r, r)]

                @pl.when(row == b)
                def _():
                    pltpu.make_async_copy(w1_ref.at[:, cols], dst, wsem.at[slot]).start()

                @pl.when(row != b)
                def _():
                    pltpu.make_async_copy(w1g.at[b, :, cols], dst, wsem.at[slot]).start()

        @pl.when(u >= n_h)
        def _():
            j = j_of((u - n_h) // n_p)
            pc = pl.ds(pl.multiple_of(lax.rem(u - n_h, n_p) * tile, tile), tile)
            pltpu.make_async_copy(w2g.at[j, :, pc], wv.at[slot], wsem.at[slot]).start()

    gamv[z] = gam_ref[...]
    gamma_sends(start)
    x_own(0, start)
    w1_own(start)
    w2_src(0, start, True)
    w1_y(0, start, True)
    x_fwd(0, 1, start, True)
    w2_src(1, start, True)
    w1_y(1, start, True)
    w1_x(0, start, True)
    x_fwd(0, 2, start, True)
    w2_src(2, start, True)
    w2_src(3, start, True)
    x_own(1, start)
    w1_y(2, start, True)
    w1_x(1, start, True)
    w1_y(3, start, True)
    w1_x(2, start, True)
    x_fwd(0, 3, start, True)
    w2_a(0, start, True)
    w1_x(3, start, True)
    far = 2 * (1 - yi) + 1 - k
    for sub in range(8):
        arrived(w1_ref_of(far, sub), w1_rv.at[far, sub])
    arrived(w1g.at[2 * yi + 1 - k], w1_ro.at[0])
    for d in range(1, 4):
        o = lax.rem(z + d, 4)
        arrived(gamv.at[o], g_rv.at[o])
    w_start(0, 0)

    events = {
        0: lambda: x_own(2, start),
        2: lambda: w2_a(1, start, True),
        4: lambda: x_fwd(1, 1, start, True),
        6: lambda: w2_a(2, start, True),
        7: lambda: (w2_b(0, start, True), w2_c(0)),
        8: lambda: (w2_a(3, start, True), x_fwd(1, 2, start, True)),
        9: lambda: (w2_b(1, start, True), w2_c(1)),
        10: lambda: (x_fwd(1, 3, start, True), x_own(3, start), x_fwd(2, 1, start, True)),
        11: lambda: (w2_b(2, start, True), w2_c(2)),
        12: lambda: (x_fwd(2, 2, start, True), x_fwd(2, 3, start, True)),
        13: lambda: (w2_b(3, start, True), w2_c(3)),
        14: lambda: (x_fwd(3, 1, start, True), x_fwd(3, 2, start, True)),
        15: lambda: x_fwd(3, 3, start, True),
    }

    def step(t, carry):
        c = t // steps
        u = lax.rem(t, steps)
        slot = lax.rem(t, 2)
        for at, ev in events.items():
            def fire(ev=ev):
                ev()

            pl.when(t == at)(fire)

        pltpu.make_async_copy(w2g.at[0, :, pl.ds(0, tile)], wv.at[slot], wsem.at[slot]).wait()

        @pl.when(t + 1 < CHUNKS * steps)
        def _():
            w_start(lax.rem(t + 1, steps), 1 - slot)

        @pl.when(u == 0)
        def _():
            normalise(c)

        sel = jnp.where(u < n_h, 0, 1)
        prod = jnp.dot(lhs[sel], wv[slot], preferred_element_type=jnp.float32)

        @pl.when(u < n_h)
        def _():
            lhs[1, :, pl.ds(pl.multiple_of(lax.rem(u, n_h) * tile, tile), tile)] = jax.nn.gelu(
                prod, approximate=True).astype(jnp.bfloat16)

        @pl.when(u >= n_h)
        def _():
            n = lax.rem(u - n_h, n_p)
            pst[:, pl.ds(pl.multiple_of(n * tile, tile), tile)] = prod

            @pl.when(n == n_p - 1)
            def _():
                j = j_of((u - n_h) // n_p)
                load(pst, pb.at[j, rows(c)], 0).wait()

                @pl.when(jnp.logical_and(z == 0, j != 0))
                def _():
                    p_send(c, 0, j, start)

                @pl.when(jnp.logical_and(z == 3, j != 3))
                def _():
                    p_send(c, 1, j, start)

        @pl.when(jnp.logical_and(u == steps - 1, c >= 1))
        def _():
            p_relay(c - 1)

        @pl.when(jnp.logical_and(u == steps - 1, c >= 2))
        def _():
            finish(c - 2)

        return carry

    lax.fori_loop(0, CHUNKS * steps, step, 0)
    p_relay(CHUNKS - 1)
    lax.fori_loop(CHUNKS - 2, CHUNKS, lambda c, s: (finish(c), s)[1], 0)

    gamma_sends(drain)
    w1_own(drain)
    for s in range(4):
        w1_y(s, drain, False)
        w1_x(s, drain, False)
        w2_src(s, drain, False)
    for i in range(4):
        w2_a(i, drain, False)
        w2_b(i, drain, False)

    def tail(c, carry):
        x_own(c, drain)
        for dist in range(1, 4):
            x_fwd(c, dist, drain, False)
        for d in range(1, 4):
            @pl.when(z == 0)
            def _():
                p_send(c, 0, d, drain)

            @pl.when(z == 3)
            def _():
                p_send(c, 1, 3 - d, drain)

        @pl.when(jnp.logical_or(z == 1, z == 2))
        def _():
            for e in range(3):
                dr, dest = inner(e)
                p_send(c, dr, dest, drain)
        return carry

    lax.fori_loop(0, CHUNKS, tail, 0)


def solution(mesh):
    tok_spec = P(("dp", "row"), "col")

    def local_block(x_loc, gamma_loc, w_in_loc, w_out_loc):
        n_tok, d_loc = x_loc.shape
        r1, hid = w_in_loc.shape
        r2 = w_out_loc.shape[0]
        bf, f32 = jnp.bfloat16, jnp.float32
        tc = n_tok // CHUNKS
        tile = 512
        sds = jax.ShapeDtypeStruct
        dma = pltpu.SemaphoreType.DMA
        any_spec = pl.BlockSpec(memory_space=pl.ANY)
        outs = pl.pallas_call(
            mlp_kernel,
            out_shape=[sds((n_tok, d_loc), bf), sds((4, n_tok, d_loc), bf), sds((4, r1, hid), bf),
                       sds((4, r2, d_loc), bf), sds((4, n_tok, d_loc), f32), sds((2, 4, n_tok, d_loc), f32)],
            in_specs=[any_spec, pl.BlockSpec(memory_space=pltpu.VMEM), any_spec, any_spec],
            out_specs=[any_spec] * 6,
            scratch_shapes=[
                pltpu.VMEM((2, tc, 4 * d_loc), bf), pltpu.VMEM((2, 4 * r1, tile), bf),
                pltpu.VMEM((4, tc, d_loc), bf), pltpu.VMEM((tc, d_loc), f32),
                pltpu.VMEM((tc, d_loc), f32), pltpu.VMEM((tc, d_loc), f32),
                pltpu.VMEM((tc, d_loc), bf), pltpu.VMEM((4, 1, d_loc), f32),
                dma((4, CHUNKS)), dma((4, CHUNKS)), dma((4, CHUNKS)), dma((4,)), dma((4,)),
                dma((1,)), dma((1,)), dma((4,)), dma((4,)), dma((8,)), dma((4, 8)),
                dma((4,)), dma((4, 2)), dma((4, 2)), dma((4, 8)), dma((4, 8)),
                dma((2, 4, CHUNKS)), dma((2, 4, CHUNKS)), dma((2,)), dma((4,)),
            ],
            compiler_params=pltpu.CompilerParams(has_side_effects=True),
            name="mlp",
        )(x_loc, gamma_loc.reshape(1, d_loc), w_in_loc, w_out_loc)
        return outs[0]

    return jax.shard_map(local_block, mesh=mesh, in_specs=(tok_spec, P("col"), P("row", "col"), P("row", "col")), out_specs=tok_spec, check_vma=False)
```

time: 1930 us -> 982 us (0.51)
  waiting for transfers between devices: 1720 us -> 0 us
  Pallas kernels: 0 us -> 972 us
  matrix products: 167 us -> 0 us
  blocking collectives: 20.5 us -> 0 us
    all_gather x4 -> x0, waiting for transfers between devices: 1720 us -> none  [the longest x1 1110 us: local_block(): h_panel = lax.all_gather(hidden, 'col', axis=1, tiled=True)]
    pallas_call x0 -> x1, Pallas kernels: none -> 972 us  [local_block(): pl.pallas_call(mlp_kernel, out_shape=[sds((n_tok, d_loc), bf), sds((4, n_...]
    dot_general x2 -> x0, matrix products: 167 us -> none  [the longest x1 87.7 us: local_block(): pre_act = jnp.dot(z_panel, w_in_panel, preferred_element_type=jnp.float32)]
    psum x1 -> x0, blocking collectives: 20.5 us -> none  [local_block(): row_sums = lax.psum(part_sums, 'col')]
  transfers between devices with their start and end apart: 4 -> 0, of which waited for: 4 -> 0; matrix products, arithmetic and copies ran while one was open for 5% -> 0% of each run, Pallas kernels for 0% -> 0%
where the time goes in v1:
time: 982 us; the launch traced here: 976 us
  Pallas kernels  972 us (99%)
    pallas_call x1, Pallas kernels, local_block(): pl.pallas_call(mlp_kernel, out_shape=[sds((n_tok, d_loc), bf), sds((4, n_...  972 us

profile of v1, /device:TPU:0, one launch (start us, length us, event | category | flops | bytes accessed | tf_op | source)
XLA Modules:
  0.0 976.3 jit_solution(10123960282321893957)
XLA Ops:
  0.0 971.7 %mlp.1 = (bf16[2048,1024]{1,0:T(8,128)(2,1)}, bf16[4,2048,1024]{2,1,0:T(8,128)(2,1)}, bf16[4,1024,4096]{2,1,0:T(8,128)(2,1)}, bf16[4,4096,1024]{2,1,0:T(8,128)(2...) custom-call(bf16[2048,1024]{1,0:T(8,128)(2,1)} %x_ref.1, f32[1,1024]{1,0:T(1,128)} %bitcast.1, ...), custom_call_target="tpu_custom_call" | custom-call | tf_op jit(solution)/shard_map/mlp/pallas_call | solution.py:428
  971.7 4.6 copy.6

commit v2 on v1

v2 whole, which is shorter than its diff:
```python
import functools

import jax
import jax.numpy as jnp
from jax import lax
from jax.experimental import pallas as pl
from jax.experimental.pallas import tpu as pltpu
from jax.sharding import PartitionSpec as P

LN_EPS = 1e-5
CHUNKS = 4
X_PARTS = 4
SWAPPED = 3
MESH = pl.DeviceIdType.MESH
SCHEDULE = (
    (-1, (("w1_own_y",), ("x_own", 3), ("x_own", 0), ("w1_own_d",), ("w1_y", 1), ("x_own", 1), ("w2_y",),
          ("x_fwd", 0, 1, 1), ("x_fwd", 0, 1, -1), ("w1_y", 2), ("w1_y", 3), ("w1_x", 2), ("x_own", 2), ("w2_z",),
          ("w1_y", 0), ("w2_i",), ("w2_a", 3), ("w2_a", 0), ("x_fwd", 0, 2, -1), ("x_fwd", 0, 2, 1), ("w2_b", 0),
          ("x_fwd", 2, 1, 1), ("x_fwd", 2, 1, -1), ("w2_a", 1), ("x_fwd", 1, 1, -1), ("x_fwd", 0, 3, 1), ("w1_x", 1),
          ("w2_b", 1), ("w1_x", 3), ("w2_c", 0, 0), ("w2_c", 0, 1), ("w2_a", 2), ("x_fwd", 0, 3, -1), ("x_fwd", 1, 1, 1),
          ("w1_x", 0), ("w1_all",),)),
    (1, (("w2_b", 2),)),
    (3, (("x_fwd", 3, 1, 1),)),
    (7, (("w2_d", 0),)),
    (8, (("w2_c", 1, 0),)),
    (9, (("w2_c", 1, 1), ("x_fwd", 1, 2, -1), ("w2_d", 1),)),
    (11, (("w2_c", 2, 0), ("w2_c", 2, 1), ("x_fwd", 2, 2, -1), ("x_fwd", 2, 2, 1), ("w2_d", 2),)),
    (13, (("x_fwd", 3, 1, -1), ("x_fwd", 1, 2, 1), ("w2_b", 3), ("w2_c", 3, 0), ("w2_c", 3, 1), ("x_fwd", 3, 2, 1),
          ("w2_d", 3), ("x_fwd", 2, 3, 1),)),
    (14, (("x_fwd", 1, 3, -1), ("x_fwd", 1, 3, 1),)),
    (16, (("p_relay", 0, 0),)),
    (24, (("x_fwd", 3, 2, -1), ("x_fwd", 2, 3, -1), ("p_relay", 0, 1), ("x_fwd", 3, 3, 1),)),
    (32, (("p_relay", 0, 2), ("p_relay", 1, 0),)),
    (36, (("p_relay", 0, 3), ("p_relay", 1, 1),)),
    (48, (("x_fwd", 3, 3, -1),)),
    (56, (("p_relay", 1, 2), ("p_relay", 2, 0), ("p_relay", 2, 1), ("p_relay", 1, 3),)),
    (64, (("p_swap", 0), ("p_relay", 2, 2), ("p_relay", 3, 0), ("p_relay", 2, 3), ("p_relay", 3, 2), ("p_swap", 1),
          ("p_relay", 3, 1), ("finish", 1), ("finish", 2), ("p_swap", 2), ("finish", 0), ("finish", 3),)),
)


def mlp_kernel(x_ref, gam_ref, w1_ref, w2_ref,
               y_ref, xg, w1g, w2g, w2t, pb, rb, yo,
               lhs, wv, xs, pst, st_a, st_b, yst, gamv,
               xs_r, xs_l, x_rv, g_sd, g_rv,
               w1_so, w1_ro, w1_sy, w1_sx, w1_sd, w1_rv,
               w2_sy, w2_sz, w2_si, w2_rt, w2_ay, w2_ax, w2_bx, w2_sd, w2_rv,
               rs_sd, rs_rv, y_sd, y_rv, wsem, lsem):
    n_tok, d_loc = x_ref.shape
    d_hid = w1_ref.shape[1]
    d_model = 4 * d_loc
    tc = n_tok // CHUNKS
    xc = n_tok // X_PARTS
    tile = wv.shape[2]
    n_h = d_hid // tile
    n_p = d_loc // tile
    steps = n_h + 4 * n_p
    w1_rows = w1_ref.shape[0] // 8
    w2_rows = w2_ref.shape[0] // 8

    xi = lax.axis_index("dp")
    z = lax.axis_index("col")
    row = lax.axis_index("row")
    yi = row // 2
    k = row % 2
    right, left = {"col": z + 1}, {"col": z - 1}
    partner = {"row": 2 * yi + 1 - k}
    y_nb = {"row": 2 * (1 - yi) + k}
    x_nb = {"dp": 1 - xi}

    def rc(src, dst, ssem, rsem, dev):
        return pltpu.make_async_remote_copy(src_ref=src, dst_ref=dst, send_sem=ssem, recv_sem=rsem,
                                            device_id=dev, device_id_type=MESH)

    def arrived(dst, rsem):
        rc(dst, dst, lsem.at[0], rsem, partner).wait_recv()

    def start(d):
        d.start()

    def drain(d):
        d.wait_send()

    def rows(c):
        return pl.ds(pl.multiple_of(c * tc, tc), tc)

    def x_rows(c):
        return pl.ds(pl.multiple_of(c * xc, xc), xc)

    def x_own(c, act=start):
        @pl.when(z < 3)
        def _():
            act(rc(x_ref.at[x_rows(c)], xg.at[z, x_rows(c)], xs_r.at[z, c], x_rv.at[z, c], right))

        @pl.when(z > 0)
        def _():
            act(rc(x_ref.at[x_rows(c)], xg.at[z, x_rows(c)], xs_l.at[z, c], x_rv.at[z, c], left))

    def x_fwd(c, dist, side, act=start, wait=True):
        s = z - side * dist
        ok = s >= 0 if side > 0 else s <= 3
        more = z < 3 if side > 0 else z > 0
        sems, to = (xs_r, right) if side > 0 else (xs_l, left)

        @pl.when(ok)
        def _():
            ref = xg.at[s, x_rows(c)]
            if wait:
                arrived(ref, x_rv.at[s, c])

            @pl.when(more)
            def _():
                act(rc(ref, ref, sems.at[s, c], x_rv.at[s, c], to))

    def gamma_sends(act):
        for d in range(1, 4):
            o = lax.rem(z + d, 4)
            act(rc(gam_ref, gamv.at[z], g_sd.at[d], g_rv.at[z], {"col": o}))

    def w1_ref_of(blk, sub):
        return w1g.at[blk, pl.ds(pl.multiple_of(sub * w1_rows, w1_rows), w1_rows)]

    def w1_own_y(act=start):
        for s in range(4):
            sub = xi * 4 + s
            src = w1_ref.at[pl.ds(pl.multiple_of(sub * w1_rows, w1_rows), w1_rows)]
            act(rc(src, w1_ref_of(row, sub), w1_sy.at[s], w1_rv.at[row, sub], y_nb))

    def w1_own_d(act=start):
        act(rc(w1_ref, w1g.at[row], w1_so.at[0], w1_ro.at[0], partner))

    def w1_y(s, act=start, wait=True):
        blk, sub = 2 * (1 - yi) + k, xi * 4 + s
        ref = w1_ref_of(blk, sub)
        if wait:
            arrived(ref, w1_rv.at[blk, sub])
        act(rc(ref, ref, w1_sx.at[s], w1_rv.at[blk, sub], x_nb))
        act(rc(ref, ref, w1_sd.at[sub], w1_rv.at[blk, sub], partner))

    def w1_x(s, act=start, wait=True):
        blk, sub = 2 * (1 - yi) + k, (1 - xi) * 4 + s
        ref = w1_ref_of(blk, sub)
        if wait:
            arrived(ref, w1_rv.at[blk, sub])
        act(rc(ref, ref, w1_sd.at[sub], w1_rv.at[blk, sub], partner))

    def w1_all():
        far = 2 * (1 - yi) + 1 - k
        for sub in range(8):
            arrived(w1_ref_of(far, sub), w1_rv.at[far, sub])
        arrived(w1g.at[2 * yi + 1 - k], w1_ro.at[0])

    def w2_rows_of(sub):
        return pl.ds(pl.multiple_of(sub * w2_rows, w2_rows), w2_rows)

    def eighth(a, b, c):
        return a * 4 + b * 2 + c

    def w2_y(act=start):
        for ks in range(2):
            sub = eighth(xi, 1 - yi, ks)
            src, dev = w2_ref.at[w2_rows_of(sub)], {"row": 2 * (1 - yi) + ks}

            @pl.when(row == z)
            def _():
                act(rc(src, w2g.at[z, w2_rows_of(sub)], w2_sy.at[ks], w2_rv.at[z, sub], dev))

            @pl.when(row != z)
            def _():
                act(rc(src, w2t.at[k], w2_sy.at[ks], w2_rt.at[k], dev))

    def w2_z(act=start, local=True):
        for ks in range(2):
            sub = eighth(xi, yi, ks)
            src, dst = w2_ref.at[w2_rows_of(sub)], w2g.at[z, w2_rows_of(sub)]
            here = jnp.logical_and(row == z, k == ks)

            @pl.when(jnp.logical_not(here))
            def _():
                act(rc(src, dst, w2_sz.at[ks], w2_rv.at[z, sub], {"row": 2 * yi + ks, "col": row}))

            if local:
                @pl.when(here)
                def _():
                    pltpu.make_async_copy(src, dst, w2_rv.at[z, sub]).start()

    def w2_i(act=start, wait=True):
        for c in range(2):
            b = 2 * (1 - yi) + c
            sub = eighth(xi, yi, k)

            @pl.when(b != z)
            def _():
                if wait:
                    arrived(w2t.at[c], w2_rt.at[c])
                act(rc(w2t.at[c], w2g.at[z, w2_rows_of(sub)], w2_si.at[c], w2_rv.at[z, sub], {"col": b}))

    def j_first(i):
        return jnp.where(z < 2, lax.rem(z + 1 + i, 4), 3 - lax.rem(4 - z + i, 4))

    def j_of(i, c):
        return jnp.where(c == 0, j_first(i), jnp.where(z < 2, 3 - i, i))

    def w2_a(i, act=start, wait=True):
        j, sub = j_first(i), eighth(xi, yi, k)
        ref, rv = w2g.at[j, w2_rows_of(sub)], w2_rv.at[j, sub]
        if wait:
            arrived(ref, rv)
        act(rc(ref, ref, w2_ay.at[j], rv, y_nb))
        act(rc(ref, ref, w2_ax.at[j], rv, x_nb))
        act(rc(ref, ref, w2_sd.at[j, sub], rv, partner))

    def w2_b(i, act=start, wait=True):
        j, sub = j_first(i), eighth(xi, 1 - yi, k)
        ref, rv = w2g.at[j, w2_rows_of(sub)], w2_rv.at[j, sub]
        if wait:
            arrived(ref, rv)
        act(rc(ref, ref, w2_bx.at[j], rv, x_nb))
        act(rc(ref, ref, w2_sd.at[j, sub], rv, partner))

    def w2_c(i, hh, act=start, wait=True):
        j, sub = j_first(i), eighth(1 - xi, 1 - yi if hh else yi, k)
        ref, rv = w2g.at[j, w2_rows_of(sub)], w2_rv.at[j, sub]
        if wait:
            arrived(ref, rv)
        act(rc(ref, ref, w2_sd.at[j, sub], rv, partner))

    def w2_d(i):
        j = j_first(i)
        for a in range(2):
            for b in range(2):
                sub = eighth(a, b, 1 - k)
                arrived(w2g.at[j, w2_rows_of(sub)], w2_rv.at[j, sub])

    def p_send(c, dr, dest, act):
        act(rc(pb.at[dest, rows(c)], rb.at[dr, dest, rows(c)], rs_sd.at[dr, dest, c],
               rs_rv.at[dr, dest, c], {"col": z + 1 - 2 * dr}))

    def load(src, dst, sem):
        d = pltpu.make_async_copy(src, dst, lsem.at[sem])
        d.start()
        return d

    def inner(e):
        m = z == 1
        if e == 0:
            return jnp.where(m, 0, 1), jnp.where(m, 3, 0)
        if e == 1:
            return jnp.where(m, 0, 1), jnp.where(m, 2, 1)
        if e == 3:
            return jnp.where(m, 1, 0), jnp.where(m, 1, 2)
        return jnp.where(m, 1, 0), jnp.where(m, 0, 3)

    def add_b():
        def part(r, carry):
            rr = pl.ds(pl.multiple_of(r * 64, 64), 64)
            st_a[rr, :] = st_a[rr, :] + st_b[rr, :]
            return carry

        lax.fori_loop(0, tc // 64, part, 0)

    def add_x():
        def part(r, carry):
            rr = pl.ds(pl.multiple_of(r * 64, 64), 64)
            yst[rr, :] = (yst[rr, :].astype(jnp.float32) + st_a[rr, :]).astype(jnp.bfloat16)
            return carry

        lax.fori_loop(0, tc // 64, part, 0)

    def p_relay(c, e):
        @pl.when(jnp.logical_or(z == 1, z == 2))
        def _():
            dr, dest = inner(e)
            d2 = load(pb.at[dest, rows(c)], st_b, 2)
            arrived(rb.at[dr, dest, rows(c)], rs_rv.at[dr, dest, c])
            d1 = load(rb.at[dr, dest, rows(c)], st_a, 1)
            d2.wait()
            d1.wait()
            add_b()
            load(st_a, pb.at[dest, rows(c)], 1).wait()
            p_send(c, dr, dest, start)

    def y_send(c, act):
        act(rc(yo.at[rows(c)], y_ref.at[rows(c)], y_sd.at[c], y_rv.at[c], {"col": jnp.where(z == 0, 1, 2)}))

    def p_swap(c):
        @pl.when(jnp.logical_or(z == 0, z == 3))
        def _():
            dr, dest = jnp.where(z == 0, 1, 0), jnp.where(z == 0, 1, 2)
            d2 = load(pb.at[dest, rows(c)], st_b, 2)
            d3 = load(xg.at[dest, rows(c)], yst, 3)
            arrived(rb.at[dr, dest, rows(c)], rs_rv.at[dr, dest, c])
            d1 = load(rb.at[dr, dest, rows(c)], st_a, 1)
            d2.wait()
            d3.wait()
            d1.wait()
            add_b()
            add_x()
            load(yst, yo.at[rows(c)], 1).wait()
            y_send(c, start)

    def finish_own(c):
        d1 = load(pb.at[z, rows(c)], st_a, 1)
        d2 = load(x_ref.at[rows(c)], yst, 2)
        d1.wait()
        d2.wait()

        @pl.when(z > 0)
        def _():
            arrived(rb.at[0, z, rows(c)], rs_rv.at[0, z, c])
            load(rb.at[0, z, rows(c)], st_b, 1).wait()
            add_b()

        @pl.when(z < 3)
        def _():
            arrived(rb.at[1, z, rows(c)], rs_rv.at[1, z, c])
            load(rb.at[1, z, rows(c)], st_b, 1).wait()
            add_b()

        add_x()
        load(yst, y_ref.at[rows(c)], 1).wait()

    def finish(c):
        if c >= SWAPPED:
            finish_own(c)
        else:
            @pl.when(jnp.logical_or(z == 0, z == 3))
            def _():
                finish_own(c)

            @pl.when(jnp.logical_or(z == 1, z == 2))
            def _():
                arrived(y_ref.at[rows(c)], y_rv.at[c])

    def normalise(c):
        for s in range(4):
            @pl.when(z == s)
            def _():
                pltpu.make_async_copy(x_ref.at[rows(c)], xs.at[s], lsem.at[3]).start()

            @pl.when(z != s)
            def _():
                pltpu.make_async_copy(xg.at[s, rows(c)], xs.at[s], lsem.at[3]).start()
        pltpu.make_async_copy(xg.at[:, rows(c)], xs, lsem.at[3]).wait()
        blk = 64

        def part(r, carry):
            rr = pl.ds(pl.multiple_of(r * blk, blk), blk)
            tot = jnp.zeros((blk, 1), jnp.float32)
            sq = jnp.zeros((blk, 1), jnp.float32)
            for s in range(4):
                v = xs[s, rr, :].astype(jnp.float32)
                tot = tot + jnp.sum(v, axis=1, keepdims=True)
                sq = sq + jnp.sum(v * v, axis=1, keepdims=True)
            mean = tot / d_model
            var = sq / d_model - mean * mean
            inv = lax.rsqrt(var + LN_EPS)
            for s in range(4):
                v = xs[s, rr, :].astype(jnp.float32)
                lhs[0, rr, s * d_loc:(s + 1) * d_loc] = ((v - mean) * inv * gamv[s]).astype(jnp.bfloat16)
            return carry

        lax.fori_loop(0, tc // blk, part, 0)

    def w_start(t, slot):
        u, c = lax.rem(t, steps), t // steps
        cols = pl.ds(pl.multiple_of(lax.rem(u, n_h) * tile, tile), tile)

        @pl.when(u < n_h)
        def _():
            r = w1_ref.shape[0]
            for b in range(4):
                dst = wv.at[slot, pl.ds(b * r, r)]

                @pl.when(row == b)
                def _():
                    pltpu.make_async_copy(w1_ref.at[:, cols], dst, wsem.at[slot]).start()

                @pl.when(row != b)
                def _():
                    pltpu.make_async_copy(w1g.at[b, :, cols], dst, wsem.at[slot]).start()

        @pl.when(u >= n_h)
        def _():
            j = j_of((u - n_h) // n_p, c)
            pc = pl.ds(pl.multiple_of(lax.rem(u - n_h, n_p) * tile, tile), tile)
            pltpu.make_async_copy(w2g.at[j, :, pc], wv.at[slot], wsem.at[slot]).start()

    table = {f.__name__: f for f in (
        x_own, x_fwd, w1_own_y, w1_own_d, w1_y, w1_x, w1_all, w2_y, w2_z, w2_i, w2_a, w2_b, w2_c, w2_d,
        p_relay, p_swap, finish)}

    def do(items):
        for it in items:
            table[it[0]](*it[1:])

    gamv[z] = gam_ref[...]
    gamma_sends(start)
    do(SCHEDULE[0][1])
    for d in range(1, 4):
        o = lax.rem(z + d, 4)
        arrived(gamv.at[o], g_rv.at[o])
    w_start(0, 0)

    def step(t, carry):
        c = t // steps
        u = lax.rem(t, steps)
        slot = lax.rem(t, 2)
        for at, items in SCHEDULE[1:-1]:
            pl.when(t == at)(functools.partial(do, items))

        pltpu.make_async_copy(w2g.at[0, :, pl.ds(0, tile)], wv.at[slot], wsem.at[slot]).wait()

        @pl.when(t + 1 < CHUNKS * steps)
        def _():
            w_start(t + 1, 1 - slot)

        @pl.when(u == 0)
        def _():
            normalise(c)

        sel = jnp.where(u < n_h, 0, 1)
        prod = jnp.dot(lhs[sel], wv[slot], preferred_element_type=jnp.float32)

        @pl.when(u < n_h)
        def _():
            lhs[1, :, pl.ds(pl.multiple_of(lax.rem(u, n_h) * tile, tile), tile)] = jax.nn.gelu(
                prod, approximate=True).astype(jnp.bfloat16)

        @pl.when(u >= n_h)
        def _():
            n = lax.rem(u - n_h, n_p)
            pst[:, pl.ds(pl.multiple_of(n * tile, tile), tile)] = prod

            @pl.when(n == n_p - 1)
            def _():
                j = j_of((u - n_h) // n_p, c)
                load(pst, pb.at[j, rows(c)], 0).wait()

                @pl.when((z == 0) & (j != 0) & ((j != 1) | (c >= SWAPPED)))
                def _():
                    p_send(c, 0, j, start)

                @pl.when((z == 3) & (j != 3) & ((j != 2) | (c >= SWAPPED)))
                def _():
                    p_send(c, 1, j, start)

        return carry

    lax.fori_loop(0, CHUNKS * steps, step, 0)
    do(SCHEDULE[-1][1])

    gamma_sends(drain)
    w1_own_y(drain)
    w1_own_d(drain)
    w2_y(drain)
    w2_z(drain, False)
    w2_i(drain, False)
    for s in range(4):
        w1_y(s, drain, False)
        w1_x(s, drain, False)
        w2_a(s, drain, False)
        w2_b(s, drain, False)
        w2_c(s, 0, drain, False)
        w2_c(s, 1, drain, False)

    def x_tail(c, carry):
        x_own(c, drain)
        for dist in range(1, 4):
            x_fwd(c, dist, 1, drain, False)
            x_fwd(c, dist, -1, drain, False)
        return carry

    lax.fori_loop(0, X_PARTS, x_tail, 0)

    def p_tail(c, carry):
        kept = c >= SWAPPED
        for d in range(1, 4):
            sent = kept if d == 1 else True

            @pl.when(jnp.logical_and(z == 0, sent))
            def _():
                p_send(c, 0, d, drain)

            @pl.when(jnp.logical_and(z == 3, sent))
            def _():
                p_send(c, 1, 3 - d, drain)

        @pl.when(jnp.logical_or(z == 1, z == 2))
        def _():
            for e in range(3):
                dr, dest = inner(e)
                p_send(c, dr, dest, drain)

        @pl.when(jnp.logical_and(jnp.logical_or(z == 1, z == 2), jnp.logical_not(kept)))
        def _():
            dr, dest = inner(3)
            p_send(c, dr, dest, drain)

        @pl.when(jnp.logical_and(jnp.logical_or(z == 0, z == 3), jnp.logical_not(kept)))
        def _():
            y_send(c, drain)

        return carry

    lax.fori_loop(0, CHUNKS, p_tail, 0)


def solution(mesh):
    tok_spec = P(("dp", "row"), "col")

    def local_block(x_loc, gamma_loc, w_in_loc, w_out_loc):
        n_tok, d_loc = x_loc.shape
        r1, hid = w_in_loc.shape
        r2 = w_out_loc.shape[0]
        bf, f32 = jnp.bfloat16, jnp.float32
        tc = n_tok // CHUNKS
        tile = 512
        sds = jax.ShapeDtypeStruct
        dma = pltpu.SemaphoreType.DMA
        any_spec = pl.BlockSpec(memory_space=pl.ANY)
        outs = pl.pallas_call(
            mlp_kernel,
            out_shape=[sds((n_tok, d_loc), bf), sds((4, n_tok, d_loc), bf), sds((4, r1, hid), bf),
                       sds((4, r2, d_loc), bf), sds((2, r2 // 8, d_loc), bf), sds((4, n_tok, d_loc), f32),
                       sds((2, 4, n_tok, d_loc), f32), sds((n_tok, d_loc), bf)],
            in_specs=[any_spec, pl.BlockSpec(memory_space=pltpu.VMEM), any_spec, any_spec],
            out_specs=[any_spec] * 8,
            scratch_shapes=[
                pltpu.VMEM((2, tc, 4 * d_loc), bf), pltpu.VMEM((2, 4 * r1, tile), bf),
                pltpu.VMEM((4, tc, d_loc), bf), pltpu.VMEM((tc, d_loc), f32),
                pltpu.VMEM((tc, d_loc), f32), pltpu.VMEM((tc, d_loc), f32),
                pltpu.VMEM((tc, d_loc), bf), pltpu.VMEM((4, 1, d_loc), f32),
                dma((4, X_PARTS)), dma((4, X_PARTS)), dma((4, X_PARTS)), dma((4,)), dma((4,)),
                dma((1,)), dma((1,)), dma((4,)), dma((4,)), dma((8,)), dma((4, 8)),
                dma((2,)), dma((2,)), dma((2,)), dma((2,)), dma((4,)), dma((4,)), dma((4,)), dma((4, 8)), dma((4, 8)),
                dma((2, 4, CHUNKS)), dma((2, 4, CHUNKS)), dma((CHUNKS,)), dma((CHUNKS,)), dma((2,)), dma((4,)),
            ],
            compiler_params=pltpu.CompilerParams(has_side_effects=True),
            name="mlp",
        )(x_loc, gamma_loc.reshape(1, d_loc), w_in_loc, w_out_loc)
        return outs[0]

    return jax.shard_map(local_block, mesh=mesh, in_specs=(tok_spec, P("col"), P("row", "col"), P("row", "col")), out_specs=tok_spec, check_vma=False)
```

time: 982 us -> 814 us (0.83)
  Pallas kernels: 972 us -> 808 us
    pallas_call x1, Pallas kernels: 972 us -> 808 us  [local_block(): pl.pallas_call(mlp_kernel, out_shape=[sds((n_tok, d_loc), bf), sds((4, n_...]
where the time goes in v2:
time: 814 us; the launch traced here: 813 us
  Pallas kernels  808 us (99%)
    pallas_call x1, Pallas kernels, local_block(): pl.pallas_call(mlp_kernel, out_shape=[sds((n_tok, d_loc), bf), sds((4, n_...  808 us

profile of v2, /device:TPU:0, one launch (start us, length us, event | category | flops | bytes accessed | tf_op | source)
XLA Modules:
  0.0 813.1 jit_solution(2867299817815937458)
XLA Ops:
  0.0 808.5 %mlp.1 = (bf16[2048,1024]{1,0:T(8,128)(2,1)}, bf16[4,2048,1024]{2,1,0:T(8,128)(2,1)}, bf16[4,1024,4096]{2,1,0:T(8,128)(2,1)}, bf16[4,4096,1024]{2,1,0:T(8,128)(2...) custom-call(bf16[2048,1024]{1,0:T(8,128)(2,1)} %x_ref.1, ...), custom_call_target="tpu_custom_call" | custom-call | tf_op jit(solution)/shard_map/mlp/pallas_call | solution.py:522
  808.5 4.6 copy.6

commit v3 on v2

--- a/solution.py
+++ b/solution.py
@@ -12,30 +12,49 @@
 X_PARTS = 4
 SWAPPED = 3
 MESH = pl.DeviceIdType.MESH
-SCHEDULE = (
-    (-1, (("w1_own_y",), ("x_own", 3), ("x_own", 0), ("w1_own_d",), ("w1_y", 1), ("x_own", 1), ("w2_y",),
-          ("x_fwd", 0, 1, 1), ("x_fwd", 0, 1, -1), ("w1_y", 2), ("w1_y", 3), ("w1_x", 2), ("x_own", 2), ("w2_z",),
-          ("w1_y", 0), ("w2_i",), ("w2_a", 3), ("w2_a", 0), ("x_fwd", 0, 2, -1), ("x_fwd", 0, 2, 1), ("w2_b", 0),
-          ("x_fwd", 2, 1, 1), ("x_fwd", 2, 1, -1), ("w2_a", 1), ("x_fwd", 1, 1, -1), ("x_fwd", 0, 3, 1), ("w1_x", 1),
-          ("w2_b", 1), ("w1_x", 3), ("w2_c", 0, 0), ("w2_c", 0, 1), ("w2_a", 2), ("x_fwd", 0, 3, -1), ("x_fwd", 1, 1, 1),
-          ("w1_x", 0), ("w1_all",),)),
-    (1, (("w2_b", 2),)),
-    (3, (("x_fwd", 3, 1, 1),)),
-    (7, (("w2_d", 0),)),
-    (8, (("w2_c", 1, 0),)),
-    (9, (("w2_c", 1, 1), ("x_fwd", 1, 2, -1), ("w2_d", 1),)),
-    (11, (("w2_c", 2, 0), ("w2_c", 2, 1), ("x_fwd", 2, 2, -1), ("x_fwd", 2, 2, 1), ("w2_d", 2),)),
-    (13, (("x_fwd", 3, 1, -1), ("x_fwd", 1, 2, 1), ("w2_b", 3), ("w2_c", 3, 0), ("w2_c", 3, 1), ("x_fwd", 3, 2, 1),
-          ("w2_d", 3), ("x_fwd", 2, 3, 1),)),
-    (14, (("x_fwd", 1, 3, -1), ("x_fwd", 1, 3, 1),)),
-    (16, (("p_relay", 0, 0),)),
-    (24, (("x_fwd", 3, 2, -1), ("x_fwd", 2, 3, -1), ("p_relay", 0, 1), ("x_fwd", 3, 3, 1),)),
-    (32, (("p_relay", 0, 2), ("p_relay", 1, 0),)),
-    (36, (("p_relay", 0, 3), ("p_relay", 1, 1),)),
-    (48, (("x_fwd", 3, 3, -1),)),
-    (56, (("p_relay", 1, 2), ("p_relay", 2, 0), ("p_relay", 2, 1), ("p_relay", 1, 3),)),
-    (64, (("p_swap", 0), ("p_relay", 2, 2), ("p_relay", 3, 0), ("p_relay", 2, 3), ("p_relay", 3, 2), ("p_swap", 1),
-          ("p_relay", 3, 1), ("finish", 1), ("finish", 2), ("p_swap", 2), ("finish", 0), ("finish", 3),)),
+END_PLANES = (
+    (-1, ("w1_own_y:2", "w1_own_d", "x_own:3", "w1_own_y:3", "x_own:0", "w1_own_y:1", "w1_own_y:0",
+          "w1_y:2", "w1_y:3", "x_fwd:0:1:-1", "w1_y:1", "w2_y:1", "x_fwd:0:1:1", "x_own:1",
+          "w1_y:0", "w1_x:2", "w1_x:3", "w2_a:1", "w2_y:0", "w2_z:1", "w2_b:1", "w2_i:0",
+          "w2_i:1", "x_fwd:0:2:1", "w2_z:0", "w1_x:0", "w1_x:1", "w1_all", "w2_a:0", "w2_b:0",
+          "w2_c:0:0", "x_fwd:0:3:1", "w2_a:2", "x_fwd:0:2:-1", "w2_c:0:1", "w2_d:0",
+          "x_fwd:0:3:-1",)),
+    (2, ("w2_c:1:0", "w2_c:1:1",)),
+    (4, ("x_fwd:1:1:1", "x_own:2", "w2_b:2",)),
+    (7, ("x_fwd:2:1:1",)),
+    (9, ("w2_c:2:0", "w2_d:1",)),
+    (10, ("x_fwd:1:1:-1",)),
+    (11, ("x_fwd:3:1:-1", "w2_c:2:1", "w2_a:3", "w2_d:2",)),
+    (12, ("x_fwd:1:2:-1", "x_fwd:1:3:-1", "x_fwd:1:2:1", "x_fwd:2:1:-1", "w2_b:3", "w2_c:3:0",)),
+    (13, ("w2_c:3:1", "w2_d:3",)),
+    (16, ("x_fwd:1:3:1",)),
+    (28, ("x_fwd:2:2:-1",)),
+    (32, ("x_fwd:3:1:1", "x_fwd:2:2:1", "x_fwd:2:3:1", "x_fwd:2:3:-1",)),
+    (48, ("x_fwd:3:2:-1", "x_fwd:3:3:-1", "p_swap:0", "x_fwd:3:2:1", "finish:0", "x_fwd:3:3:1",)),
+    (64, ("finish:1", "finish:2", "p_swap:1", "p_swap:2", "finish:3",)),
+)
+INNER_PLANES = (
+    (-1, ("x_own:0", "w1_own_y:1", "w2_z:1", "w1_own_y:0", "w2_y:1", "w2_z:0", "x_own:2",
+          "w2_y:0", "w1_own_y:3", "w1_y:0", "w1_own_d", "x_fwd:0:1:1", "x_fwd:0:1:-1", "w2_a:3",
+          "w2_i:0", "w2_i:1", "w1_own_y:2", "w1_y:1", "w1_y:3", "w2_a:0", "x_own:1",
+          "x_fwd:0:2:-1", "w2_b:3", "w1_y:2", "x_fwd:0:2:1", "x_fwd:0:3:1", "w2_a:1",
+          "w2_b:0", "w2_b:1", "x_own:3", "x_fwd:1:1:-1", "x_fwd:1:2:-1", "w2_c:0:0", "w1_x:2",
+          "w2_a:2", "x_fwd:1:1:1", "w1_x:0", "x_fwd:3:1:-1", "w2_b:2", "x_fwd:2:1:1",
+          "w2_c:0:1", "w1_x:3", "x_fwd:1:2:1", "x_fwd:2:1:-1", "x_fwd:3:1:1", "x_fwd:0:3:-1",
+          "w2_c:1:0", "x_fwd:3:2:-1", "x_fwd:3:3:-1", "w1_x:1", "w1_all",)),
+    (2, ("x_fwd:3:2:1", "x_fwd:2:2:-1", "w2_c:3:0", "w2_c:3:1",)),
+    (6, ("w2_c:1:1",)),
+    (7, ("w2_d:0", "x_fwd:1:3:-1", "w2_c:2:0", "w2_c:2:1", "w2_d:2", "w2_d:1",)),
+    (11, ("w2_d:3", "x_fwd:2:2:1",)),
+    (16, ("p_relay:0:1", "x_fwd:2:3:-1", "x_fwd:1:3:1",)),
+    (28, ("p_relay:0:0", "p_relay:0:3",)),
+    (32, ("p_relay:1:0", "x_fwd:2:3:1",)),
+    (36, ("p_relay:0:2",)),
+    (48, ("p_relay:1:1", "p_relay:2:0", "p_relay:1:2", "p_relay:1:3", "p_relay:2:1",
+          "x_fwd:3:3:1",)),
+    (60, ("p_relay:2:2", "finish:0",)),
+    (64, ("p_relay:3:0", "p_relay:2:3", "p_relay:3:1", "p_relay:3:2", "finish:1", "finish:2",
+          "finish:3",)),
 )
 
 
@@ -63,6 +82,8 @@
     row = lax.axis_index("row")
     yi = row // 2
     k = row % 2
+    at_end = jnp.logical_or(z == 0, z == 3)
+    inside = jnp.logical_not(at_end)
     right, left = {"col": z + 1}, {"col": z - 1}
     partner = {"row": 2 * yi + 1 - k}
     y_nb = {"row": 2 * (1 - yi) + k}
@@ -86,6 +107,11 @@
 
     def x_rows(c):
         return pl.ds(pl.multiple_of(c * xc, xc), xc)
+
+    def load(src, dst, sem):
+        d = pltpu.make_async_copy(src, dst, lsem.at[sem])
+        d.start()
+        return d
 
     def x_own(c, act=start):
         @pl.when(z < 3)
@@ -120,11 +146,10 @@
     def w1_ref_of(blk, sub):
         return w1g.at[blk, pl.ds(pl.multiple_of(sub * w1_rows, w1_rows), w1_rows)]
 
-    def w1_own_y(act=start):
-        for s in range(4):
-            sub = xi * 4 + s
-            src = w1_ref.at[pl.ds(pl.multiple_of(sub * w1_rows, w1_rows), w1_rows)]
-            act(rc(src, w1_ref_of(row, sub), w1_sy.at[s], w1_rv.at[row, sub], y_nb))
+    def w1_own_y(s, act=start):
+        sub = xi * 4 + s
+        src = w1_ref.at[pl.ds(pl.multiple_of(sub * w1_rows, w1_rows), w1_rows)]
+        act(rc(src, w1_ref_of(row, sub), w1_sy.at[s], w1_rv.at[row, sub], y_nb))
 
     def w1_own_d(act=start):
         act(rc(w1_ref, w1g.at[row], w1_so.at[0], w1_ro.at[0], partner))
@@ -156,44 +181,42 @@
     def eighth(a, b, c):
         return a * 4 + b * 2 + c
 
-    def w2_y(act=start):
-        for ks in range(2):
-            sub = eighth(xi, 1 - yi, ks)
-            src, dev = w2_ref.at[w2_rows_of(sub)], {"row": 2 * (1 - yi) + ks}
-
-            @pl.when(row == z)
-            def _():
-                act(rc(src, w2g.at[z, w2_rows_of(sub)], w2_sy.at[ks], w2_rv.at[z, sub], dev))
-
-            @pl.when(row != z)
-            def _():
-                act(rc(src, w2t.at[k], w2_sy.at[ks], w2_rt.at[k], dev))
-
-    def w2_z(act=start, local=True):
-        for ks in range(2):
-            sub = eighth(xi, yi, ks)
-            src, dst = w2_ref.at[w2_rows_of(sub)], w2g.at[z, w2_rows_of(sub)]
-            here = jnp.logical_and(row == z, k == ks)
-
-            @pl.when(jnp.logical_not(here))
-            def _():
-                act(rc(src, dst, w2_sz.at[ks], w2_rv.at[z, sub], {"row": 2 * yi + ks, "col": row}))
-
-            if local:
-                @pl.when(here)
-                def _():
-                    pltpu.make_async_copy(src, dst, w2_rv.at[z, sub]).start()
-
-    def w2_i(act=start, wait=True):
-        for c in range(2):
-            b = 2 * (1 - yi) + c
-            sub = eighth(xi, yi, k)
-
-            @pl.when(b != z)
-            def _():
-                if wait:
-                    arrived(w2t.at[c], w2_rt.at[c])
-                act(rc(w2t.at[c], w2g.at[z, w2_rows_of(sub)], w2_si.at[c], w2_rv.at[z, sub], {"col": b}))
+    def w2_y(ks, act=start):
+        sub = eighth(xi, 1 - yi, ks)
+        src, dev = w2_ref.at[w2_rows_of(sub)], {"row": 2 * (1 - yi) + ks}
+
+        @pl.when(row == z)
+        def _():
+            act(rc(src, w2g.at[z, w2_rows_of(sub)], w2_sy.at[ks], w2_rv.at[z, sub], dev))
+
+        @pl.when(row != z)
+        def _():
+            act(rc(src, w2t.at[k], w2_sy.at[ks], w2_rt.at[k], dev))
+
+    def w2_z(ks, act=start, local=True):
+        sub = eighth(xi, yi, ks)
+        src, dst = w2_ref.at[w2_rows_of(sub)], w2g.at[z, w2_rows_of(sub)]
+        here = jnp.logical_and(row == z, k == ks)
+
+        @pl.when(jnp.logical_not(here))
+        def _():
+            act(rc(src, dst, w2_sz.at[ks], w2_rv.at[z, sub], {"row": 2 * yi + ks, "col": row}))
+
+        if local:
+            @pl.when(here)
+            def _():
+                load(src, yst.at[pl.ds(0, w2_rows)], 2).wait()
+                pltpu.make_async_copy(yst.at[pl.ds(0, w2_rows)], dst, w2_rv.at[z, sub]).start()
+
+    def w2_i(c, act=start, wait=True):
+        b = 2 * (1 - yi) + c
+        sub = eighth(xi, yi, k)
+
+        @pl.when(b != z)
+        def _():
+            if wait:
+                arrived(w2t.at[c], w2_rt.at[c])
+            act(rc(w2t.at[c], w2g.at[z, w2_rows_of(sub)], w2_si.at[c], w2_rv.at[z, sub], {"col": b}))
 
     def j_first(i):
         return jnp.where(z < 2, lax.rem(z + 1 + i, 4), 3 - lax.rem(4 - z + i, 4))
@@ -235,11 +258,6 @@
     def p_send(c, dr, dest, act):
         act(rc(pb.at[dest, rows(c)], rb.at[dr, dest, rows(c)], rs_sd.at[dr, dest, c],
                rs_rv.at[dr, dest, c], {"col": z + 1 - 2 * dr}))
-
-    def load(src, dst, sem):
-        d = pltpu.make_async_copy(src, dst, lsem.at[sem])
-        d.start()
-        return d
 
     def inner(e):
         m = z == 1
@@ -392,11 +410,13 @@
 
     def do(items):
         for it in items:
-            table[it[0]](*it[1:])
+            name, *args = it.split(":")
+            table[name](*map(int, args))
 
     gamv[z] = gam_ref[...]
     gamma_sends(start)
-    do(SCHEDULE[0][1])
+    pl.when(at_end)(functools.partial(do, END_PLANES[0][1]))
+    pl.when(inside)(functools.partial(do, INNER_PLANES[0][1]))
     for d in range(1, 4):
         o = lax.rem(z + d, 4)
         arrived(gamv.at[o], g_rv.at[o])
@@ -406,8 +426,9 @@
         c = t // steps
         u = lax.rem(t, steps)
         slot = lax.rem(t, 2)
-        for at, items in SCHEDULE[1:-1]:
-            pl.when(t == at)(functools.partial(do, items))
+        for mine, plan in ((at_end, END_PLANES), (inside, INNER_PLANES)):
+            for at, items in plan[1:-1]:
+                pl.when(jnp.logical_and(mine, t == at))(functools.partial(do, items))
 
         pltpu.make_async_copy(w2g.at[0, :, pl.ds(0, tile)], wv.at[slot], wsem.at[slot]).wait()
 
@@ -448,15 +469,17 @@
         return carry
 
     lax.fori_loop(0, CHUNKS * steps, step, 0)
-    do(SCHEDULE[-1][1])
+    pl.when(at_end)(functools.partial(do, END_PLANES[-1][1]))
+    pl.when(inside)(functools.partial(do, INNER_PLANES[-1][1]))
 
     gamma_sends(drain)
-    w1_own_y(drain)
     w1_own_d(drain)
-    w2_y(drain)
-    w2_z(drain, False)
-    w2_i(drain, False)
+    for s in range(2):
+        w2_y(s, drain)
+        w2_z(s, drain, False)
+        w2_i(s, drain, False)
     for s in range(4):
+        w1_own_y(s, drain)
         w1_y(s, drain, False)
         w1_x(s, drain, False)
         w2_a(s, drain, False)
@@ -530,7 +553,7 @@
                 pltpu.VMEM((2, tc, 4 * d_loc), bf), pltpu.VMEM((2, 4 * r1, tile), bf),
                 pltpu.VMEM((4, tc, d_loc), bf), pltpu.VMEM((tc, d_loc), f32),
                 pltpu.VMEM((tc, d_loc), f32), pltpu.VMEM((tc, d_loc), f32),
-                pltpu.VMEM((tc, d_loc), bf), pltpu.VMEM((4, 1, d_loc), f32),
+                pltpu.VMEM((max(tc, r2 // 8), d_loc), bf), pltpu.VMEM((4, 1, d_loc), f32),
                 dma((4, X_PARTS)), dma((4, X_PARTS)), dma((4, X_PARTS)), dma((4,)), dma((4,)),
                 dma((1,)), dma((1,)), dma((4,)), dma((4,)), dma((8,)), dma((4, 8)),
                 dma((2,)), dma((2,)), dma((2,)), dma((2,)), dma((4,)), dma((4,)), dma((4,)), dma((4, 8)), dma((4, 8)),

time: 814 us -> 756 us (0.929)
  Pallas kernels: 808 us -> 744 us
    pallas_call x1, Pallas kernels: 808 us -> 744 us  [local_block(): pl.pallas_call(mlp_kernel, out_shape=[sds((n_tok, d_loc), bf), sds((4, n_...]
where the time goes in v3:
time: 756 us; the launch traced here: 749 us
  Pallas kernels  744 us (98%)
    pallas_call x1, Pallas kernels, local_block(): pl.pallas_call(mlp_kernel, out_shape=[sds((n_tok, d_loc), bf), sds((4, n_...  744 us

profile of v3, /device:TPU:0, one launch (start us, length us, event | category | flops | bytes accessed | tf_op | source)
XLA Modules:
  0.0 748.5 jit_solution(6562053097201625920)
XLA Ops:
  0.0 743.9 %mlp.1 = (bf16[2048,1024]{1,0:T(8,128)(2,1)}, bf16[4,2048,1024]{2,1,0:T(8,128)(2,1)}, bf16[4,1024,4096]{2,1,0:T(8,128)(2,1)}, bf16[4,4096,1024]{2,1,0:T(8,128)(2...) custom-call(bf16[2048,1024]{1,0:T(8,128)(2,1)} %x_ref.1, ...), custom_call_target="tpu_custom_call" | custom-call | tf_op jit(solution)/shard_map/mlp/pallas_call | solution.py:545
  743.9 4.6 copy.6
